TPU v7x, 32 devices: a whole 2x2x4 slice. The times are simulated.
32 devices in a mesh: dp: 4 (over y, core), vocab: 8 (over z, x).
Axes of the slice: x: 2, y: 2, z: 4, core: 2. Of those that a mesh axis runs over, the one named last changes fastest.
Arguments:
- hidden: bfloat16 [256, 3584], P('dp'), may hold values from -48 to 48
- embedding: bfloat16 [24576, 3584], P(('dp', 'vocab')), may hold values from -1 to 1
- targets: int32 [256], P('dp'), may hold values from 0 to 24575
- loss_weight: bfloat16 [256], P('dp'), may hold values from 1 to 10
Outputs:
- hidden_grad: bfloat16 [256, 3584], P('dp')
- table_grad: bfloat16 [24576, 3584], P(('dp', 'vocab'))
All inputs are finite; a program needn't handle non-finite values.
Results may differ from a plain program's by a relative error of at most 0.0049.
Values may be sent and summed in bfloat16 or wider, within the bound.
A program may use at most 128 MiB of HBM per device.

v0:
```python
import jax
import jax.numpy as jnp
from jax import lax
from jax.sharding import PartitionSpec as P

soft_cap = 30.0
z_weight = 0.002


def body(hidden, embedding, targets, loss_weight):
    shard_rows = embedding.shape[0]
    group_hidden, group_weight = (
        lax.all_gather(hidden, "dp", axis=0, tiled=True),
        lax.all_gather(loss_weight, "dp", axis=0, tiled=True),
    )
    group_targets = lax.all_gather(targets, "dp", axis=0, tiled=True)
    logits = lax.dot_general(
        group_hidden, embedding, (((1,), (1,)), ((), ())), preferred_element_type=jnp.float32
    )
    capped = soft_cap * jnp.tanh(logits / soft_cap)
    exp_terms = jnp.exp(capped - soft_cap)
    partial_value = jnp.sum(exp_terms, axis=1)
    weight = group_weight.astype(jnp.float32)
    device_place = lax.axis_index("dp") * lax.axis_size("vocab") + lax.axis_index("vocab")
    exp_total = lax.psum(partial_value, ("dp", "vocab"))
    factor = weight * (1.0 + 2.0 * z_weight * (soft_cap + jnp.log(exp_total))) / exp_total
    columns = device_place * shard_rows + lax.iota(jnp.int32, shard_rows)
    target_hit = group_targets[:, None] == columns[None, :]
    softmax_part = factor[:, None] * exp_terms - jnp.where(target_hit, weight[:, None], 0.0)
    scores_grad = (softmax_part * (1.0 - (capped / soft_cap) ** 2)).astype(jnp.bfloat16)
    table_grad = lax.dot_general(
        scores_grad, group_hidden, (((0,), (0,)), ((), ())), preferred_element_type=jnp.float32
    ).astype(jnp.bfloat16)
    group_grad = lax.psum_scatter(
        jnp.dot(scores_grad, embedding, preferred_element_type=jnp.float32),
        "dp",
        scatter_dimension=0,
        tiled=True,
    )
    hidden_grad = lax.psum(group_grad, "vocab").astype(jnp.bfloat16)
    return (hidden_grad, table_grad)


def solution(mesh):
    return jax.shard_map(
        body,
        mesh=mesh,
        in_specs=(P("dp", None), P(("dp", "vocab"), None), P("dp"), P("dp")),
        out_specs=(P("dp", None), P(("dp", "vocab"), None)),
        check_vma=False,
    )
```

profile of v0, /device:TPU:0, one launch (start us, length us, event | category | flops | bytes accessed | tf_op | source)
XLA Modules:
  0.0 182.5 jit_solution(10813239611045289594)
XLA Ops:
  7.2 0.0 all-gather.2.cloned.1.call-start
  7.2 0.7 all-gather.2.cloned.1.call-update
  7.9 0.0 reduce-scatter.2.cloned.1.call-start
  8.0 1.2 dynamic-slice
  9.9 0.9 dynamic-update-slice
  10.7 8.4 %all-reduce = bf16[256]{0:T(256)(128)(2,1)S(1)} all-reduce(bf16[256]{0:T(256)(128)(2,1)S(1)} %dynamic-update-slice), channel_id=1, replica_groups=mesh['dp'=4,'vocab'=8] {'dp'}, use_global_device_ids=true, to_apply=%add | all-reduce | flops 256 | bytes 1024
  19.1 0.9 dynamic-update-slice.1
  20.0 4.5 %all-reduce.1 = s32[256]{0:T(256)S(1)} all-reduce(s32[256]{0:T(256)S(1)} %dynamic-update-slice.1), channel_id=1, replica_groups=mesh['dp'=4,'vocab'=8] {'dp'}, use_global_device_ids=true, to_apply=%add.1 | all-reduce | flops 256 | bytes 2048
  24.4 9.0 %all-gather.2.cloned.1.call-done = bf16[256,3584]{1,0:T(8,128)(2,1)} async-done(((bf16[64,3584]{1,0:T(8,128)(2,1)}), bf16[256,3584]{1,0:T(8,128)(2,1)}) %all-gather.2.cloned.1.call-update) | async-done | bytes 1835024 | tf_op jit(solution)/shard_map/all_gather | solution.py:13
  33.5 4.9 %fusion.1 = (f32[256]{0:T(256)S(1)}, f32[256,768]{1,0:T(8,128)S(1)}) fusion(bf16[256,3584]{1,0:T(8,128)(2,1)} %all-gather.2.cloned.1.call-done, bf16[768,3584]{1,0:T(8,128)(2,1)} %param.5), kind=kOutput, calls=%fused_computation.5 | convolution fusion | flops 1410072320 | bytes 8127488 | tf_op jit(solution)/shard_map/dot_general | solution.py:17
  38.4 39.3 %psum.14 = f32[256]{0:T(256)S(1)} all-reduce(f32[256]{0:T(256)S(1)} %get-tuple-element.2), channel_id=1, replica_groups=mesh['dp'=4,'vocab'=8] {'dp','vocab'}, use_global_device_ids=true, to_apply=%region_1.0 | all-reduce | flops 256 | bytes 2048 | tf_op jit(solution)/shard_map/psum | solution.py:25
  77.7 0.0 copy-start
  77.7 6.3 %fusion.2 = f32[256,3584]{1,0:T(8,128)} fusion(bf16[768,3584]{1,0:T(8,128)(2,1)} %param.5, f32[256,768]{1,0:T(8,128)S(1)} %get-tuple-element.3, f32[256]{0:T(256)S(1)} %convert_element_type.12, s32[768]{0:T(1024)S(1)} %iota_add_fusion, f32[256]{0:T(256)S(1)} %multiply_divide_fusion, s32[256]{0:T(256)S(1)} %all-reduce.1), kind=kOutput, calls=%fused_computation.8 | convolution fusion | flops 1411252224 | bytes 9967616 | tf_op jit(solution)/shard_map/dot_general | solution.py:35
  84.0 0.0 reduce-scatter.2.cloned.1.call-update
  84.0 0.0 copy-done
  84.0 4.3 %convolution_convert_fusion = bf16[768,3584]{1,0:T(8,128)(2,1)} fusion(bf16[256,3584]{1,0:T(8,128)(2,1)S(1)} %copy-done, f32[256,768]{1,0:T(8,128)S(1)} %get-tuple-element.3, f32[256]{0:T(256)S(1)} %convert_element_type.12, s32[768]{0:T(1024)S(1)} %iota_add_fusion, f32[256]{0:T(256)S(1)} %multiply_divide_fusion, s32[256]{0:T(256)S(1)} %all-reduce.1), kind=kOutput, calls=%fused_computation | convolution fusion | flops 1414004736 | bytes 8132608 | tf_op jit(solution)/shard_map/dot_general | solution.py:31
  88.3 37.9 %reduce-scatter.2.cloned.1.call-done = f32[64,3584]{1,0:T(8,128)} async-done(((f32[256,3584]{1,0:T(8,128)}), f32[64,3584]{1,0:T(8,128)}) %reduce-scatter.2.cloned.1.call-update) | async-done | bytes 917520 | tf_op jit(solution)/shard_map/reduce_scatter | solution.py:34
  126.2 49.4 %all-reduce.3 = bf16[64,3584]{1,0:T(8,128)(2,1)} all-reduce(f32[64,3584]{1,0:T(8,128)} %reduce-scatter.2.cloned.1.call-done), channel_id=1, replica_groups=mesh['dp'=4,'vocab'=8] {'vocab'}, use_global_device_ids=true, to_apply=%region_3.4 | all-reduce | flops 229376 | bytes 1376256 | tf_op jit(solution)/shard_map/psum | solution.py:40
  (5 shorter events, 0.0 us)
Async XLA Ops:
  7.2 26.3 %all-gather.2.cloned.1.call-start = ((), (), s32[]{:S(2)}) async-start(), calls=%async_computation.1 | async-start | bytes 2293760 | tf_op jit(solution)/shard_map/all_gather | solution.py:13
  7.9 118.3 %reduce-scatter.2.cloned.1.call-start = ((), (), s32[]{:S(2)}) async-start(), calls=%async_computation.2 | async-start | bytes 4587520 | tf_op jit(solution)/shard_map/reduce_scatter | solution.py:34
  77.7 6.3 %copy-start = (bf16[256,3584]{1,0:T(8,128)(2,1)S(1)}, bf16[256,3584]{1,0:T(8,128)(2,1)}, u32[]{:S(2)}) copy-start(bf16[256,3584]{1,0:T(8,128)(2,1)} %all-gather.2.cloned.1.call-done) | copy-start | bytes 5505028
Sparse Core Ops, SparseCore 0:
  9.5 23.9 all-gather.1
  84.1 42.0 reduce-scatter.1
where the time goes:
time: 183 us; the launch traced here: 182 us
  blocking collectives  102 us (56%)
  waiting for transfers between devices  47.6 us (26%)
  matrix products  15.4 us (8%)
  between operations  14.7 us (8%)
  local copies, waits for them, and re-layouts  2.97 us (2%)
    psum x1, blocking collectives, body(): hidden_grad = lax.psum(group_grad, 'vocab').astype(jnp.bfloat16)  49.4 us
    psum x1, blocking collectives, body(): exp_total = lax.psum(partial_value, ('dp', 'vocab'))  39.3 us
    reduce_scatter x1, waiting for transfers between devices, body(): lax.psum_scatter(jnp.dot(scores_grad, embedding, preferred_element_type=j...  37.9 us
    unnamed x2, blocking collectives  12.8 us
    all_gather x1, waiting for transfers between devices, body(): lax.all_gather(hidden, 'dp', axis=0, tiled=True)  9.04 us
    dot_general x1, matrix products, body(): jnp.dot(scores_grad, embedding, preferred_element_type=jnp.float32)  6.28 us
    dot_general x1, matrix products, body(): lax.dot_general(group_hidden, embedding, (((1,), (1,)), ((), ())), prefer...  4.91 us
    dot_general x1, matrix products, body(): lax.dot_general(scores_grad, group_hidden, (((0,), (0,)), ((), ())), pref...  4.26 us
  transfers between devices with their start and end apart: 2, of which 2 were waited for; matrix products, arithmetic and copies ran while one was open for 4% of the time, Pallas kernels for 0%

commit v1 on v0

--- a/solution.py
+++ b/solution.py
@@ -22,7 +22,9 @@
     partial_value = jnp.sum(exp_terms, axis=1)
     weight = group_weight.astype(jnp.float32)
     device_place = lax.axis_index("dp") * lax.axis_size("vocab") + lax.axis_index("vocab")
-    exp_total = lax.psum(partial_value, ("dp", "vocab"))
+    exp_total = partial_value
+    for j0 in ("dp", "vocab"):
+        exp_total = lax.psum(exp_total, axis_name=j0)
     factor = weight * (1.0 + 2.0 * z_weight * (soft_cap + jnp.log(exp_total))) / exp_total
     columns = device_place * shard_rows + lax.iota(jnp.int32, shard_rows)
     target_hit = group_targets[:, None] == columns[None, :]

time: 183 us -> 167 us (0.913)
  blocking collectives: 102 us -> 89.6 us
  waiting for transfers between devices: 47.6 us -> 44 us
    psum x1 -> x2, blocking collectives: 39.3 us -> 27.4 us  [body(): exp_total = lax.psum(exp_total, axis_name=j0)]
    reduce_scatter x1, waiting for transfers between devices: 37.9 us -> 34.3 us  [body(): lax.psum_scatter(jnp.dot(scores_grad, embedding, preferred_element_type=j...]
where the time goes in v1:
time: 167 us
  blocking collectives  89.6 us (54%)
  waiting for transfers between devices  44 us (26%)
  matrix products  15.5 us (9%)
  between operations  14.7 us (9%)
  local copies, waits for them, and re-layouts  2.97 us (2%)
    psum x1, blocking collectives, body(): hidden_grad = lax.psum(group_grad, 'vocab').astype(jnp.bfloat16)  49.4 us
    reduce_scatter x1, waiting for transfers between devices, body(): lax.psum_scatter(jnp.dot(scores_grad, embedding, preferred_element_type=j...  34.3 us
    psum x2, blocking collectives, body(): exp_total = lax.psum(exp_total, axis_name=j0)  27.4 us
    unnamed x2, blocking collectives  12.8 us
    all_gather x1, waiting for transfers between devices, body(): lax.all_gather(hidden, 'dp', axis=0, tiled=True)  9.04 us
    dot_general x1, matrix products, body(): jnp.dot(scores_grad, embedding, preferred_element_type=jnp.float32)  6.28 us
    dot_general x1, matrix products, body(): lax.dot_general(group_hidden, embedding, (((1,), (1,)), ((), ())), prefer...  4.91 us
    dot_general x1, matrix products, body(): lax.dot_general(scores_grad, group_hidden, (((0,), (0,)), ((), ())), pref...  4.36 us
  transfers between devices with their start and end apart: 2, of which 2 were waited for; matrix products, arithmetic and copies ran while one was open for 4% of the time, Pallas kernels for 0%

profile of v1, /device:TPU:0, one launch (start us, length us, event | category | flops | bytes accessed | tf_op | source)
XLA Modules:
  0.0 167.0 jit_solution(12238479305498964102)
XLA Ops:
  7.2 0.0 all-gather.2.cloned.1.call-start
  7.2 0.7 all-gather.2.cloned.1.call-update
  7.9 0.0 reduce-scatter.2.cloned.1.call-start
  8.0 1.2 dynamic-slice
  9.9 0.9 dynamic-update-slice
  10.7 8.4 %all-reduce = bf16[256]{0:T(256)(128)(2,1)S(1)} all-reduce(bf16[256]{0:T(256)(128)(2,1)S(1)} %dynamic-update-slice), channel_id=1, replica_groups=mesh['dp'=4,'vocab'=8] {'dp'}, use_global_device_ids=true, to_apply=%add | all-reduce | flops 256 | bytes 1024
  19.1 0.9 dynamic-update-slice.1
  20.0 4.5 %all-reduce.1 = s32[256]{0:T(256)S(1)} all-reduce(s32[256]{0:T(256)S(1)} %dynamic-update-slice.1), channel_id=1, replica_groups=mesh['dp'=4,'vocab'=8] {'dp'}, use_global_device_ids=true, to_apply=%add.1 | all-reduce | flops 256 | bytes 2048
  24.4 9.0 %all-gather.2.cloned.1.call-done = bf16[256,3584]{1,0:T(8,128)(2,1)} async-done(((bf16[64,3584]{1,0:T(8,128)(2,1)}), bf16[256,3584]{1,0:T(8,128)(2,1)}) %all-gather.2.cloned.1.call-update) | async-done | bytes 1835024 | tf_op jit(solution)/shard_map/all_gather | solution.py:13
  33.5 4.9 %fusion.1 = (f32[256]{0:T(256)S(1)}, f32[256,768]{1,0:T(8,128)S(1)}) fusion(bf16[256,3584]{1,0:T(8,128)(2,1)} %all-gather.2.cloned.1.call-done, bf16[768,3584]{1,0:T(8,128)(2,1)} %param.5), kind=kOutput, calls=%fused_computation.5 | convolution fusion | flops 1410072320 | bytes 8127488 | tf_op jit(solution)/shard_map/dot_general | solution.py:17
  38.4 5.9 %psum.21 = f32[256]{0:T(256)S(1)} all-reduce(f32[256]{0:T(256)S(1)} %get-tuple-element.2), channel_id=1, replica_groups=mesh['dp'=4,'vocab'=8] {'dp'}, use_global_device_ids=true, to_apply=%region_1.0 | all-reduce | flops 256 | bytes 2048 | tf_op jit(solution)/shard_map/psum | solution.py:27
  44.3 21.5 %psum.22 = f32[256]{0:T(256)S(1)} all-reduce(f32[256]{0:T(256)S(1)} %psum.21), channel_id=1, replica_groups=mesh['dp'=4,'vocab'=8] {'vocab'}, use_global_device_ids=true, to_apply=%region_2.0 | all-reduce | flops 256 | bytes 2048 | tf_op jit(solution)/shard_map/psum | solution.py:27
  65.8 0.0 copy-start
  65.8 6.3 %fusion.2 = f32[256,3584]{1,0:T(8,128)} fusion(bf16[768,3584]{1,0:T(8,128)(2,1)} %param.5, f32[256,768]{1,0:T(8,128)S(1)} %get-tuple-element.3, f32[256]{0:T(256)S(1)} %convert_element_type.12, s32[768]{0:T(1024)S(1)} %iota_add_fusion, f32[256]{0:T(256)S(1)} %multiply_divide_fusion, s32[256]{0:T(256)S(1)} %all-reduce.1), kind=kOutput, calls=%fused_computation.8 | convolution fusion | flops 1411252224 | bytes 9967616 | tf_op jit(solution)/shard_map/dot_general | solution.py:37
  72.1 0.0 reduce-scatter.2.cloned.1.call-update
  72.1 0.0 copy-done
  72.1 4.4 %convolution_convert_fusion = bf16[768,3584]{1,0:T(8,128)(2,1)} fusion(bf16[256,3584]{1,0:T(8,128)(2,1)S(1)} %copy-done, f32[256,768]{1,0:T(8,128)S(1)} %get-tuple-element.3, f32[256]{0:T(256)S(1)} %convert_element_type.12, s32[768]{0:T(1024)S(1)} %iota_add_fusion, f32[256]{0:T(256)S(1)} %multiply_divide_fusion, s32[256]{0:T(256)S(1)} %all-reduce.1), kind=kOutput, calls=%fused_computation | convolution fusion | flops 1414004736 | bytes 8132608 | tf_op jit(solution)/shard_map/dot_general | solution.py:33
  76.4 34.3 %reduce-scatter.2.cloned.1.call-done = f32[64,3584]{1,0:T(8,128)} async-done(((f32[256,3584]{1,0:T(8,128)}), f32[64,3584]{1,0:T(8,128)}) %reduce-scatter.2.cloned.1.call-update) | async-done | bytes 917520 | tf_op jit(solution)/shard_map/reduce_scatter | solution.py:36
  110.7 49.4 %all-reduce.3 = bf16[64,3584]{1,0:T(8,128)(2,1)} all-reduce(f32[64,3584]{1,0:T(8,128)} %reduce-scatter.2.cloned.1.call-done), channel_id=1, replica_groups=mesh['dp'=4,'vocab'=8] {'vocab'}, use_global_device_ids=true, to_apply=%region_4.5 | all-reduce | flops 229376 | bytes 1376256 | tf_op jit(solution)/shard_map/psum | solution.py:42
  (5 shorter events, 0.0 us)
Async XLA Ops:
  7.2 26.3 %all-gather.2.cloned.1.call-start = ((), (), s32[]{:S(2)}) async-start(), calls=%async_computation.1 | async-start | bytes 2293760 | tf_op jit(solution)/shard_map/all_gather | solution.py:13
  7.9 102.8 %reduce-scatter.2.cloned.1.call-start = ((), (), s32[]{:S(2)}) async-start(), calls=%async_computation.2 | async-start | bytes 4587520 | tf_op jit(solution)/shard_map/reduce_scatter | solution.py:36
  65.8 6.3 %copy-start = (bf16[256,3584]{1,0:T(8,128)(2,1)S(1)}, bf16[256,3584]{1,0:T(8,128)(2,1)}, u32[]{:S(2)}) copy-start(bf16[256,3584]{1,0:T(8,128)(2,1)} %all-gather.2.cloned.1.call-done) | copy-start | bytes 5505028
Sparse Core Ops, SparseCore 0:
  9.5 23.9 all-gather.1
  72.2 38.4 reduce-scatter.1
